TPU v7x, 32 devices: a whole 2x2x4 slice. The times are simulated.
32 devices in a mesh: region: 4 (over z), depth: 2 (over y), member: 4 (over x, core).
Axes of the slice: x: 2, y: 2, z: 4, core: 2. Of those that a mesh axis runs over, the one named last changes fastest.
Arguments:
- ensemble: bfloat16 [14, 384, 4096], P('depth', 'member', 'region'), may hold values from -6 to 6
- obs_weights: float32 [14], P('depth'), may hold values from -1.5 to 1.5
- obs_tiles: int32 [2048], P('region'), may hold values from 0 to 1023
- obs_values: float32 [2048], P('region'), may hold values from -8 to 8
- obs_error: float32 [2048], P('region'), may hold values from 0.2 to 2
- obs_noise: float32 [384, 2048], P('member', 'region'), may hold values from -6 to 6
Outputs:
- analysis: bfloat16 [14, 384, 4096], P('depth', 'member', 'region')
- inflation: float32 [], replicated
Inputs may be any that keep to these rules, and one draw needn't show every extreme that they name: `obs_tiles`: the tile of the observation, counted within the 1024 tiles of the region whose block holds the observation.
All inputs are finite; a program needn't handle non-finite values.
Results may differ from a plain program's by a relative error of at most 0.011.
Values may be sent and summed in bfloat16 or wider, within the bound.
A program may use at most 64 MiB of HBM per device.

v0:
```python
import jax
import jax.numpy as jnp
from jax import lax
from jax.sharding import PartitionSpec as P

MEMBERS = 384
RADIUS = 1024


def extended(array, sides, width):
    for axis, dim in sides:
        peers, length = (lax.axis_size(axis), array.shape[dim])
        up = [(i, (i + 1) % peers) for i in range(peers - 1)]
        down = [(j, i) for i, j in up]
        last = lax.slice_in_dim(array, length - width, length, axis=dim)
        leading = lax.slice_in_dim(array, 0, width, axis=dim)
        before = lax.ppermute(last, axis, up)
        after = lax.ppermute(leading, axis, down)
        array = jnp.concatenate([before, array, after], axis=dim)
    return array


def regress(
    anomalies, own_anom, state_mean, obs_anom, perturbed, factor, obs_pos, first_tile, infl_root
):
    var_count = anomalies.shape[0]
    tile_count = anomalies.shape[2]
    block = 128

    def one_block(block_index, output):
        block_start = block_index * block
        slab = lax.dynamic_slice_in_dim(anomalies, block_start, block, 2)
        own_slab = lax.dynamic_slice_in_dim(own_anom, block_start, block, 2)
        means = lax.dynamic_slice_in_dim(state_mean, block_start, block, 1)
        covariance = jnp.einsum(
            "lmt,mj->ltj", slab, obs_anom, preferred_element_type=jnp.float32
        ) / (MEMBERS - 1)
        tile_pos = (first_tile + block_start + jnp.arange(block, dtype=jnp.int32)).astype(
            jnp.float32
        )
        closeness = jnp.maximum(0.0, 1.0 - jnp.abs(tile_pos[:, None] - obs_pos[None, :]) / RADIUS)
        kalman_gain = (covariance * (closeness * closeness * factor[None, :])[None]).astype(
            jnp.bfloat16
        )
        increment = jnp.einsum(
            "ltj,mj->lmt", kalman_gain, perturbed, preferred_element_type=jnp.float32
        )
        updated = (means[:, None, :] + infl_root * own_slab.astype(jnp.float32) + increment).astype(
            jnp.bfloat16
        )
        return lax.dynamic_update_slice_in_dim(output, updated, block_start, 2)

    output = jnp.zeros((var_count, perturbed.shape[0], tile_count), jnp.bfloat16)
    return lax.fori_loop(0, tile_count // block, one_block, output)


def shards(ensemble, obs_weights, obs_tiles, obs_values, obs_error, obs_noise):
    tile_count = ensemble.shape[2]
    own_members = ensemble.shape[1]
    obs_count = obs_tiles.shape[0]
    member_sum = jnp.sum(ensemble, axis=1, dtype=jnp.float32)
    picked = jnp.take(ensemble, obs_tiles, axis=2).astype(jnp.float32)
    partial_pred = jnp.einsum("lmk,l->mk", picked, obs_weights, precision=lax.Precision.HIGHEST)
    predicted = lax.psum(partial_pred, "depth")
    totals = lax.psum(
        (member_sum, jnp.sum(predicted, axis=0), jnp.sum(predicted * predicted, axis=0)), "member"
    )
    state_mean = totals[0] / MEMBERS
    obs_mean = totals[1] / MEMBERS
    obs_dev = predicted - obs_mean[None, :]
    obs_spread = (totals[2] - MEMBERS * obs_mean * obs_mean) / (MEMBERS - 1)
    innovation = obs_values - obs_mean
    global_sums = lax.psum(
        (jnp.sum(innovation * innovation), jnp.sum(obs_spread + obs_error)), "region"
    )
    inflation = global_sums[0] / global_sums[1]
    infl_root = jnp.sqrt(inflation)
    factor = inflation / (inflation * obs_spread + obs_error)
    obs_anom = obs_dev.astype(jnp.bfloat16)
    perturbed = (
        innovation[None, :] + jnp.sqrt(obs_error)[None, :] * obs_noise - infl_root * obs_dev
    ).astype(jnp.bfloat16)
    first_tile = lax.axis_index("region") * tile_count
    obs_pos = (first_tile + obs_tiles).astype(jnp.float32)
    stacked = jnp.concatenate([obs_anom, perturbed], axis=0)
    widened = extended(stacked, (("region", 1),), obs_count)
    near_anom = widened[:own_members]
    near_pert = widened[own_members:]
    scalars = jnp.stack([factor, obs_pos], axis=0)
    wide_scalars = extended(scalars, (("region", 1),), obs_count)
    near_factor = wide_scalars[0]
    near_pos = wide_scalars[1]
    anomalies = (ensemble.astype(jnp.float32) - state_mean[:, None, :]).astype(jnp.bfloat16)
    all_anom, all_obs_anom = (
        lax.all_gather(anomalies, "member", axis=1, tiled=True),
        lax.all_gather(near_anom, "member", axis=0, tiled=True),
    )
    analysis = regress(
        all_anom,
        anomalies,
        state_mean,
        all_obs_anom,
        near_pert,
        near_factor,
        near_pos,
        first_tile,
        infl_root,
    )
    return (analysis, inflation)


def solution(mesh):
    return jax.shard_map(
        shards,
        mesh=mesh,
        in_specs=(
            P("depth", "member", "region"),
            P("depth"),
            P("region"),
            P("region"),
            P("region"),
            P("member", "region"),
        ),
        out_specs=(P("depth", "member", "region"), P()),
        check_vma=False,
    )
```

profile of v0, /device:TPU:0, one launch (start us, length us, event | category | flops | bytes accessed | tf_op | source)
XLA Modules:
  0.0 185.1 jit_solution(7628334277064460269)
XLA Ops:
  8.6 3.2 %copy.8 = bf16[7,96,1024]{1,0,2:T(8,128)(2,1)S(1)} copy(bf16[7,96,1024]{2,1,0:T(8,128)(2,1)} %param.8) | data formatting | bytes 2752512 | tf_op args[0]
  11.8 1.8 gather_fusion
  13.7 1.8 select_bitcast_fusion
  15.4 1.0 copy.9
  16.5 0.8 fusion.20
  17.3 0.7 copy.12
  18.4 25.0 %all-reduce.4.cloned.1.call-done = f32[96,512]{1,0:T(8,128)} async-done(((f32[96,512]{1,0:T(8,128)}), f32[96,512]{1,0:T(8,128)}) %all-reduce.4.cloned.1.call-update) | async-done | bytes 196624 | tf_op jit(solution)/shard_map/psum | solution.py:64
  43.3 1.0 multiply_reduce_fusion
  44.3 10.8 %all-reduce = (f32[7,1024]{1,0:T(8,128)S(1)}, f32[512]{0:T(512)S(1)}, f32[512]{0:T(512)S(1)}) all-reduce(f32[7,1024]{1,0:T(8,128)S(1)} %convert_reduce_fusion, f32[512]{0:T(512)S(1)} %get-tuple-element.188, f32[512]{0:T(512)S(1)} %get-tuple-element.187), channel_id=1, replica_groups=mesh['region'=4,'depth'=2,'member'=4] {'member'}, use_global_device_ids=true, to_apply=%region_1.2 | all-reduce | flops 8192 | bytes 65536 | tf_op jit(solution)/shard_map/psum | solution.py:65
  55.7 12.3 %all-reduce.1 = (f32[]{:T(128)}, f32[]{:T(128)}) all-reduce(f32[]{:T(128)} %get-tuple-element.216, f32[]{:T(128)} %get-tuple-element.229), channel_id=1, replica_groups=mesh['region'=4,'depth'=2,'member'=4] {'region'}, use_global_device_ids=true, to_apply=%region_6.7 | all-reduce | flops 2 | bytes 16 | tf_op jit(solution)/shard_map/psum | solution.py:73
  69.5 1.0 subtract_convert_fusion.1
  70.5 1.3 collective-permute-start.1
  71.8 4.6 %collective-permute-start = (bf16[192,512]{1,0:T(8,128)(2,1)S(1)}, bf16[192,512]{1,0:T(8,128)(2,1)S(1)}, u32[]{:S(2)}, u32[]{:S(2)}) collective-permute-start(bf16[192,512]{1,0:T(8,128)(2,1)S(1)} %pad_maximum_fusion.1), channel_id=1, source_target_pairs={{0,8},{8,16},{16,24},{1,9},{9,17},{17,25},{2,10},{10,18},{18,26},{... | collective-permute-start | bytes 589832 | tf_op jit(solution)/shard_map/ppermute | solution.py:17
  76.4 1.7 collective-permute-done.1
  78.1 1.5 collective-permute-done
  79.6 0.8 fusion.23
  80.4 1.4 fusion.18
  81.9 1.3 collective-permute-start.3
  83.2 5.0 %collective-permute-start.2 = (f32[2,512]{1,0:T(2,128)S(1)}, f32[2,512]{1,0:T(2,128)S(1)}, u32[]{:S(2)}, u32[]{:S(2)}) collective-permute-start(f32[2,512]{1,0:T(2,128)S(1)} %pad_maximum_fusion.3), channel_id=1, source_target_pairs={{0,8},{8,16},{16,24},{1,9},{9,17},{17,25},{2,10},{10,18},{18,26},{... | collective-permute-start | bytes 12296 | tf_op jit(solution)/shard_map/ppermute | solution.py:17
  88.2 1.3 collective-permute-done.2
  89.6 7.4 %all-gather.5.cloned.1.call-done = bf16[384,1536]{1,0:T(8,128)(2,1)} async-done(((bf16[96,1536]{1,0:T(8,128)(2,1)}), bf16[384,1536]{1,0:T(8,128)(2,1)}) %all-gather.5.cloned.1.call-update) | async-done | bytes 1179664 | tf_op jit(solution)/shard_map/all_gather | solution.py:96
  97.0 44.1 %all-gather.3.cloned.1.call-done = bf16[7,384,1024]{2,1,0:T(8,128)(2,1)} async-done(((bf16[7,96,1024]{2,1,0:T(8,128)(2,1)}), bf16[7,384,1024]{2,1,0:T(8,128)(2,1)}) %all-gather.3.cloned.1.call-update) | async-done | bytes 5505040 | tf_op jit(solution)/shard_map/all_gather | solution.py:95
  141.2 35.1 %while.13 = (s32[]{:T(128)}, bf16[7,96,1024]{2,1,0:T(8,128)(2,1)S(1)}, f32[7,1024]{1,0:T(8,128)S(1)}, f32[]{:T(128)}, bf16[7,96,1024]{2,1,0:T(8,128)(2,1)}, /*in...) while((s32[]{:T(128)}, ...), condition=%wide.region_12.13_spmd, body=%wide.region_11.12_spmd.sunk | while | flops 1325961472 | bytes 4130527 | solution.py:54
  141.6 4.0 %fusion.33 = bf16[7,96,1024]{2,1,0:T(8,128)(2,1)S(1)} fusion(bf16[7,96,1024]{2,1,0:T(8,128)(2,1)S(1)} %get-tuple-element.314, s32[]{:T(128)S(6)} %select_n.27, f32[128,1536]{1,0:T(8,128)S(1)} %multiply_multiply_fusion.2, bf16[384,1536]{1,0:T(8,128)(2,1)} %get-tuple-element.335, bf16[7,384,1024]{2,1,0:T(8,128)(2,1)} %get-tuple-element.334, ...), kind=kOutput, calls=%fused_computation.7.clone.1 | convolution fusion | flops 1324388352 | bytes 3298816 | tf_op jit(solution)/shard_map/while/body/eval_jaxpr/ltj,mj->lmt/dot_general | solution.py:45
  146.0 4.0 %fusion.33 = bf16[7,96,1024]{2,1,0:T(8,128)(2,1)S(1)} fusion(bf16[7,96,1024]{2,1,0:T(8,128)(2,1)S(1)} %get-tuple-element.314, s32[]{:T(128)S(6)} %select_n.27, f32[128,1536]{1,0:T(8,128)S(1)} %multiply_multiply_fusion.2, bf16[384,1536]{1,0:T(8,128)(2,1)} %get-tuple-element.335, bf16[7,384,1024]{2,1,0:T(8,128)(2,1)} %get-tuple-element.334, ...), kind=kOutput, calls=%fused_computation.7.clone.1 | convolution fusion | flops 1324388352 | bytes 3298816 | tf_op jit(solution)/shard_map/while/body/eval_jaxpr/ltj,mj->lmt/dot_general | solution.py:45
  150.4 4.0 %fusion.33 = bf16[7,96,1024]{2,1,0:T(8,128)(2,1)S(1)} fusion(bf16[7,96,1024]{2,1,0:T(8,128)(2,1)S(1)} %get-tuple-element.314, s32[]{:T(128)S(6)} %select_n.27, f32[128,1536]{1,0:T(8,128)S(1)} %multiply_multiply_fusion.2, bf16[384,1536]{1,0:T(8,128)(2,1)} %get-tuple-element.335, bf16[7,384,1024]{2,1,0:T(8,128)(2,1)} %get-tuple-element.334, ...), kind=kOutput, calls=%fused_computation.7.clone.1 | convolution fusion | flops 1324388352 | bytes 3298816 | tf_op jit(solution)/shard_map/while/body/eval_jaxpr/ltj,mj->lmt/dot_general | solution.py:45
  154.8 4.0 %fusion.33 = bf16[7,96,1024]{2,1,0:T(8,128)(2,1)S(1)} fusion(bf16[7,96,1024]{2,1,0:T(8,128)(2,1)S(1)} %get-tuple-element.314, s32[]{:T(128)S(6)} %select_n.27, f32[128,1536]{1,0:T(8,128)S(1)} %multiply_multiply_fusion.2, bf16[384,1536]{1,0:T(8,128)(2,1)} %get-tuple-element.335, bf16[7,384,1024]{2,1,0:T(8,128)(2,1)} %get-tuple-element.334, ...), kind=kOutput, calls=%fused_computation.7.clone.1 | convolution fusion | flops 1324388352 | bytes 3298816 | tf_op jit(solution)/shard_map/while/body/eval_jaxpr/ltj,mj->lmt/dot_general | solution.py:45
  159.2 4.0 %fusion.33 = bf16[7,96,1024]{2,1,0:T(8,128)(2,1)S(1)} fusion(bf16[7,96,1024]{2,1,0:T(8,128)(2,1)S(1)} %get-tuple-element.314, s32[]{:T(128)S(6)} %select_n.27, f32[128,1536]{1,0:T(8,128)S(1)} %multiply_multiply_fusion.2, bf16[384,1536]{1,0:T(8,128)(2,1)} %get-tuple-element.335, bf16[7,384,1024]{2,1,0:T(8,128)(2,1)} %get-tuple-element.334, ...), kind=kOutput, calls=%fused_computation.7.clone.1 | convolution fusion | flops 1324388352 | bytes 3298816 | tf_op jit(solution)/shard_map/while/body/eval_jaxpr/ltj,mj->lmt/dot_general | solution.py:45
  163.6 4.0 %fusion.33 = bf16[7,96,1024]{2,1,0:T(8,128)(2,1)S(1)} fusion(bf16[7,96,1024]{2,1,0:T(8,128)(2,1)S(1)} %get-tuple-element.314, s32[]{:T(128)S(6)} %select_n.27, f32[128,1536]{1,0:T(8,128)S(1)} %multiply_multiply_fusion.2, bf16[384,1536]{1,0:T(8,128)(2,1)} %get-tuple-element.335, bf16[7,384,1024]{2,1,0:T(8,128)(2,1)} %get-tuple-element.334, ...), kind=kOutput, calls=%fused_computation.7.clone.1 | convolution fusion | flops 1324388352 | bytes 3298816 | tf_op jit(solution)/shard_map/while/body/eval_jaxpr/ltj,mj->lmt/dot_general | solution.py:45
  167.9 4.0 %fusion.33 = bf16[7,96,1024]{2,1,0:T(8,128)(2,1)S(1)} fusion(bf16[7,96,1024]{2,1,0:T(8,128)(2,1)S(1)} %get-tuple-element.314, s32[]{:T(128)S(6)} %select_n.27, f32[128,1536]{1,0:T(8,128)S(1)} %multiply_multiply_fusion.2, bf16[384,1536]{1,0:T(8,128)(2,1)} %get-tuple-element.335, bf16[7,384,1024]{2,1,0:T(8,128)(2,1)} %get-tuple-element.334, ...), kind=kOutput, calls=%fused_computation.7.clone.1 | convolution fusion | flops 1324388352 | bytes 3298816 | tf_op jit(solution)/shard_map/while/body/eval_jaxpr/ltj,mj->lmt/dot_general | solution.py:45
  172.3 4.0 %fusion.33 = bf16[7,96,1024]{2,1,0:T(8,128)(2,1)S(1)} fusion(bf16[7,96,1024]{2,1,0:T(8,128)(2,1)S(1)} %get-tuple-element.314, s32[]{:T(128)S(6)} %select_n.27, f32[128,1536]{1,0:T(8,128)S(1)} %multiply_multiply_fusion.2, bf16[384,1536]{1,0:T(8,128)(2,1)} %get-tuple-element.335, bf16[7,384,1024]{2,1,0:T(8,128)(2,1)} %get-tuple-element.334, ...), kind=kOutput, calls=%fused_computation.7.clone.1 | convolution fusion | flops 1324388352 | bytes 3298816 | tf_op jit(solution)/shard_map/while/body/eval_jaxpr/ltj,mj->lmt/dot_general | solution.py:45
  176.4 1.1 copy-done.2
  (71 shorter events, 5.4 us)
Async XLA Ops:
  7.2 9.3 %copy-start = (f32[7]{0:T(128)S(1)}, f32[7]{0:T(128)}, u32[]{:S(2)}) copy-start(f32[7]{0:T(128)} %param.9) | copy-start | bytes 88
  7.2 36.1 %all-reduce.4.cloned.1.call-start = ((), (), s32[]{:S(2)}) async-start(), calls=%async_computation | async-start | bytes 393216 | tf_op jit(solution)/shard_map/psum | solution.py:64
  15.4 2.6 %copy-start.1 = (bf16[7,96,1024]{2,1,0:T(8,128)(2,1)S(1)}, bf16[7,96,1024]{2,1,0:T(8,128)(2,1)}, u32[]{:S(2)}) copy-start(bf16[7,96,1024]{2,1,0:T(8,128)(2,1)} %param.8) | copy-start | bytes 4128772
  16.5 38.6 %copy-start.4 = (f32[512]{0:T(512)S(1)}, f32[512]{0:T(512)}, u32[]{:S(2)}) copy-start(f32[512]{0:T(512)} %param.12) | copy-start | bytes 6148
  16.5 38.6 %copy-start.5 = (f32[512]{0:T(512)S(1)}, f32[512]{0:T(512)}, u32[]{:S(2)}) copy-start(f32[512]{0:T(512)} %param.11) | copy-start | bytes 6148
  17.3 52.2 %copy-start.3 = (f32[96,512]{1,0:T(8,128)S(1)}, f32[96,512]{1,0:T(8,128)}, u32[]{:S(2)}) copy-start(f32[96,512]{1,0:T(8,128)} %param.13) | copy-start | bytes 589828
  18.0 79.0 %all-gather.5.cloned.1.call-start = ((), (), s32[]{:S(2)}) async-start(), calls=%async_computation.2 | async-start | bytes 1474560 | tf_op jit(solution)/shard_map/all_gather | solution.py:96
  70.5 7.6 %collective-permute-start.1 = (bf16[192,512]{1,0:T(8,128)(2,1)S(1)}, bf16[192,512]{1,0:T(8,128)(2,1)S(1)}, u32[]{:S(2)}, u32[]{:S(2)}) collective-permute-start(bf16[192,512]{1,0:T(8,128)(2,1)S(1)} %pad_maximum_fusion.1), channel_id=1, source_target_pairs={{8,0},{16,8},{24,16},{9,1},{17,9},{25,17},{10,2},{18,10},{26,18},{... | collective-permute-start | bytes 589832 | tf_op jit(solution)/shard_map/ppermute | solution.py:18
  71.8 7.7 %collective-permute-start = (bf16[192,512]{1,0:T(8,128)(2,1)S(1)}, bf16[192,512]{1,0:T(8,128)(2,1)S(1)}, u32[]{:S(2)}, u32[]{:S(2)}) collective-permute-start(bf16[192,512]{1,0:T(8,128)(2,1)S(1)} %pad_maximum_fusion.1), channel_id=1, source_target_pairs={{0,8},{8,16},{16,24},{1,9},{9,17},{17,25},{2,10},{10,18},{18,26},{... | collective-permute-start | bytes 589832 | tf_op jit(solution)/shard_map/ppermute | solution.py:17
  80.4 60.7 %all-gather.3.cloned.1.call-start = ((), (), s32[]{:S(2)}) async-start(), calls=%async_computation.1 | async-start | bytes 6881280 | tf_op jit(solution)/shard_map/all_gather | solution.py:95
  81.9 6.3 %collective-permute-start.3 = (f32[2,512]{1,0:T(2,128)S(1)}, f32[2,512]{1,0:T(2,128)S(1)}, u32[]{:S(2)}, u32[]{:S(2)}) collective-permute-start(f32[2,512]{1,0:T(2,128)S(1)} %pad_maximum_fusion.3), channel_id=1, source_target_pairs={{8,0},{16,8},{24,16},{9,1},{17,9},{25,17},{10,2},{18,10},{26,18},{... | collective-permute-start | bytes 12296 | tf_op jit(solution)/shard_map/ppermute | solution.py:18
  83.2 6.3 %collective-permute-start.2 = (f32[2,512]{1,0:T(2,128)S(1)}, f32[2,512]{1,0:T(2,128)S(1)}, u32[]{:S(2)}, u32[]{:S(2)}) collective-permute-start(f32[2,512]{1,0:T(2,128)S(1)} %pad_maximum_fusion.3), channel_id=1, source_target_pairs={{0,8},{8,16},{16,24},{1,9},{9,17},{17,25},{2,10},{10,18},{18,26},{... | collective-permute-start | bytes 12296 | tf_op jit(solution)/shard_map/ppermute | solution.py:17
  176.3 1.1 copy-start.2
Sparse Core Ops, SparseCore 0:
  18.1 25.1 all-reduce.3
  80.5 16.4 all-gather.4
  99.1 41.8 all-gather.2
where the time goes:
time: 186 us; the launch traced here: 185 us
  waiting for transfers between devices  80.9 us (43%)
  matrix products  32.7 us (18%)
  blocking collectives  23.2 us (12%)
  between operations  16.5 us (9%)
  starting transfers between devices  12.3 us (7%)
  other arithmetic  10.1 us (5%)
  local copies, waits for them, and re-layouts  8.89 us (5%)
    all_gather x1, waiting for transfers between devices, shards(): lax.all_gather(anomalies, 'member', axis=1, tiled=True)  44.1 us
    dot_general x8, matrix products, one_block(): jnp.einsum('ltj,mj->lmt', kalman_gain, perturbed, preferred_element_type=...  31.9 us
    psum x1, waiting for transfers between devices, shards(): predicted = lax.psum(partial_pred, 'depth')  25 us
    psum x1, blocking collectives, shards(): lax.psum((jnp.sum(innovation * innovation), jnp.sum(obs_spread + obs_erro...  12.3 us
    psum x1, blocking collectives, shards(): lax.psum((member_sum, jnp.sum(predicted, axis=0), jnp.sum(predicted * pre...  10.8 us
    ppermute x2, starting transfers between devices, extended(): before = lax.ppermute(last, axis, up)  9.57 us
    all_gather x1, waiting for transfers between devices, shards(): lax.all_gather(near_anom, 'member', axis=0, tiled=True)  7.4 us
    unnamed x13, local copies, waits for them, and re-layouts  4.34 us
  transfers between devices with their start and end apart: 7, of which 6 were waited for; matrix products, arithmetic and copies ran while one was open for 1% of the time, Pallas kernels for 0%

commit v1 on v0

--- a/solution.py
+++ b/solution.py
@@ -92,7 +92,7 @@
     near_pos = wide_scalars[1]
     anomalies = (ensemble.astype(jnp.float32) - state_mean[:, None, :]).astype(jnp.bfloat16)
     all_anom, all_obs_anom = (
-        lax.all_gather(anomalies, "member", axis=1, tiled=True),
+        jnp.concatenate(lax.all_gather(anomalies, "member"), axis=1),
         lax.all_gather(near_anom, "member", axis=0, tiled=True),
     )
     analysis = regress(

time: 186 us -> 162 us (0.87)
  waiting for transfers between devices: 80.9 us -> 57.4 us
  local copies, waits for them, and re-layouts: 8.89 us -> 15.4 us
  starting transfers between devices: 12.3 us -> 6.7 us
    all_gather x1, waiting for transfers between devices: 44.1 us -> 8.79 us  [shards(): lax.all_gather(anomalies, 'member')]
    ppermute x2, waiting for transfers between devices: 1.7 us -> 8.59 us  [extended(): after = lax.ppermute(leading, axis, down)]
    reshape x0 -> x1, local copies, waits for them, and re-layouts: none -> 5.95 us  [shards(): jnp.concatenate(lax.all_gather(anomalies, 'member'), axis=1)]
    all_gather x1, waiting for transfers between devices: 7.4 us -> 13.1 us  [shards(): lax.all_gather(near_anom, 'member', axis=0, tiled=True)]
    ppermute x2, starting transfers between devices: 9.57 us -> 4 us  [extended(): before = lax.ppermute(last, axis, up)]
    unnamed x13 -> x15, local copies, waits for them, and re-layouts: 4.34 us -> 4.94 us
  transfers between devices with their start and end apart: 7 -> 7, of which waited for: 6 -> 6; matrix products, arithmetic and copies ran while one was open for 1% -> 5% of each run, Pallas kernels for 0% -> 0%
where the time goes in v1:
time: 162 us; the launch traced here: 161 us
  waiting for transfers between devices  57.4 us (35%)
  matrix products  32.6 us (20%)
  blocking collectives  23.2 us (14%)
  between operations  16.5 us (10%)
  local copies, waits for them, and re-layouts  15.4 us (10%)
  other arithmetic  9.15 us (6%)
  starting transfers between devices  6.7 us (4%)
    dot_general x8, matrix products, one_block(): jnp.einsum('ltj,mj->lmt', kalman_gain, perturbed, preferred_element_type=...  31.8 us
    psum x1, waiting for transfers between devices, shards(): predicted = lax.psum(partial_pred, 'depth')  25 us
    all_gather x1, waiting for transfers between devices, shards(): lax.all_gather(near_anom, 'member', axis=0, tiled=True)  13.1 us
    psum x1, blocking collectives, shards(): lax.psum((jnp.sum(innovation * innovation), jnp.sum(obs_spread + obs_erro...  12.4 us
    psum x1, blocking collectives, shards(): lax.psum((member_sum, jnp.sum(predicted, axis=0), jnp.sum(predicted * pre...  10.8 us
    all_gather x1, waiting for transfers between devices, shards(): lax.all_gather(anomalies, 'member')  8.79 us
    ppermute x2, waiting for transfers between devices, extended(): after = lax.ppermute(leading, axis, down)  8.59 us
    reshape x1, local copies, waits for them, and re-layouts, shards(): jnp.concatenate(lax.all_gather(anomalies, 'member'), axis=1)  5.95 us
  transfers between devices with their start and end apart: 7, of which 6 were waited for; matrix products, arithmetic and copies ran while one was open for 5% of the time, Pallas kernels for 0%

profile of v1, /device:TPU:0, one launch (start us, length us, event | category | flops | bytes accessed | tf_op | source)
XLA Modules:
  0.0 161.4 jit_solution(3487958056996630153)
XLA Ops:
  8.6 3.2 %copy.15 = bf16[7,96,1024]{1,0,2:T(8,128)(2,1)S(1)} copy(bf16[7,96,1024]{2,1,0:T(8,128)(2,1)} %param.8) | data formatting | bytes 2752512 | tf_op args[0]
  11.8 1.8 %gather_fusion = bf16[512,7,96]{2,1,0:T(8,128)(2,1)S(1)} fusion(bf16[7,96,1024]{1,0,2:T(8,128)(2,1)S(1)} %copy.15, s32[1024]{0:T(1024)S(1)} %pad_clamp_fusion), kind=kCustom, calls=%fused_computation | custom fusion | bytes 1378304 | tf_op jit(solution)/shard_map/jit(_take)/gather | solution.py:62
  13.7 1.8 %select_bitcast_fusion = bf16[7,96,512]{1,0,2:T(8,128)(2,1)S(1)} fusion(bf16[512,7,96]{2,1,0:T(8,128)(2,1)S(1)} %gather_fusion, pred[512]{0:T(512)(128)(4,1)S(1)} %compare_and_fusion), kind=kLoop, calls=%fused_computation.17 | loop fusion | flops 344064 | bytes 1376768 | tf_op jit(solution)/shard_map/jit(_take)/select_n | solution.py:62
  15.4 1.0 copy.18
  16.5 0.8 fusion.20
  17.3 0.7 copy.22
  18.3 25.0 %all-reduce.4.cloned.1.call-done = f32[96,512]{1,0:T(8,128)} async-done(((f32[96,512]{1,0:T(8,128)}), f32[96,512]{1,0:T(8,128)}) %all-reduce.4.cloned.1.call-update) | async-done | bytes 196624 | tf_op jit(solution)/shard_map/psum | solution.py:64
  43.3 1.0 multiply_reduce_fusion
  44.2 10.8 %all-reduce = (f32[7,1024]{1,0:T(8,128)S(1)}, f32[512]{0:T(512)S(1)}, f32[512]{0:T(512)S(1)}) all-reduce(f32[7,1024]{1,0:T(8,128)S(1)} %convert_reduce_fusion, f32[512]{0:T(512)S(1)} %get-tuple-element.210, f32[512]{0:T(512)S(1)} %get-tuple-element.209), channel_id=1, replica_groups=mesh['region'=4,'depth'=2,'member'=4] {'member'}, use_global_device_ids=true, to_apply=%region_1.2 | all-reduce | flops 8192 | bytes 65536 | tf_op jit(solution)/shard_map/psum | solution.py:65
  55.1 1.4 fusion.18
  57.9 12.4 %all-reduce.1 = (f32[]{:T(128)}, f32[]{:T(128)}) all-reduce(f32[]{:T(128)} %get-tuple-element.238, f32[]{:T(128)} %get-tuple-element.251), channel_id=1, replica_groups=mesh['region'=4,'depth'=2,'member'=4] {'region'}, use_global_device_ids=true, to_apply=%region_6.7 | all-reduce | flops 2 | bytes 16 | tf_op jit(solution)/shard_map/psum | solution.py:73
  71.8 1.3 collective-permute-start
  73.1 1.3 collective-permute-start.1
  74.4 1.9 %collective-permute-done = bf16[192,512]{1,0:T(8,128)(2,1)S(1)} collective-permute-done((bf16[192,512]{1,0:T(8,128)(2,1)S(1)}, bf16[192,512]{1,0:T(8,128)(2,1)S(1)}, u32[]{:S(2)}, u32[]{:S(2)}) %collective-permute-start) | collective-permute-done | bytes 196640 | tf_op jit(solution)/shard_map/ppermute | solution.py:17
  76.3 4.4 %collective-permute-done.1 = bf16[192,512]{1,0:T(8,128)(2,1)S(1)} collective-permute-done((bf16[192,512]{1,0:T(8,128)(2,1)S(1)}, bf16[192,512]{1,0:T(8,128)(2,1)S(1)}, u32[]{:S(2)}, u32[]{:S(2)}) %collective-permute-start.1) | collective-permute-done | bytes 196640 | tf_op jit(solution)/shard_map/ppermute | solution.py:18
  80.7 0.8 fusion.23
  81.5 2.7 %collective-permute-start.2 = (f32[2,512]{1,0:T(2,128)S(1)}, f32[2,512]{1,0:T(2,128)S(1)}, u32[]{:S(2)}, u32[]{:S(2)}) collective-permute-start(f32[2,512]{1,0:T(2,128)S(1)} %pad_maximum_fusion.3), channel_id=1, source_target_pairs={{0,8},{8,16},{16,24},{1,9},{9,17},{17,25},{2,10},{10,18},{18,26},{... | collective-permute-start | bytes 12296 | tf_op jit(solution)/shard_map/ppermute | solution.py:17
  84.2 1.3 collective-permute-start.3
  85.5 4.2 %collective-permute-done.3 = f32[2,512]{1,0:T(2,128)S(1)} collective-permute-done((f32[2,512]{1,0:T(2,128)S(1)}, f32[2,512]{1,0:T(2,128)S(1)}, u32[]{:S(2)}, u32[]{:S(2)}) %collective-permute-start.3) | collective-permute-done | bytes 4128 | tf_op jit(solution)/shard_map/ppermute | solution.py:18
  89.7 8.8 %all-gather.6.cloned.1.call-done = bf16[28,96,1024]{2,1,0:T(8,128)(2,1)} async-done(((bf16[7,96,1024]{2,1,0:T(8,128)(2,1)}), bf16[28,96,1024]{2,1,0:T(8,128)(2,1)}) %all-gather.6.cloned.1.call-update) | async-done | bytes 5505040 | tf_op jit(solution)/shard_map/all_gather | solution.py:95
  98.5 5.9 %copy.16 = bf16[7,4,96,1024]{3,2,1,0:T(8,128)(2,1)} copy(bf16[7,4,96,1024]{3,2,0,1:T(8,128)(2,1)} %bitcast.42) | data formatting | bytes 11010048 | tf_op jit(solution)/shard_map/reshape | solution.py:95
  104.5 13.1 %all-gather.4.cloned.1.call-done = bf16[384,1536]{1,0:T(8,128)(2,1)} async-done(((bf16[96,1536]{1,0:T(8,128)(2,1)}), bf16[384,1536]{1,0:T(8,128)(2,1)}) %all-gather.4.cloned.1.call-update) | async-done | bytes 1179664 | tf_op jit(solution)/shard_map/all_gather | solution.py:96
  117.7 35.0 %while.13 = (s32[]{:T(128)}, bf16[7,96,1024]{2,1,0:T(8,128)(2,1)S(1)}, f32[7,1024]{1,0:T(8,128)S(1)}, f32[]{:T(128)}, bf16[7,96,1024]{2,1,0:T(8,128)(2,1)}, /*in...) while((s32[]{:T(128)}, ...), condition=%wide.region_12.13_spmd, body=%wide.region_11.12_spmd.sunk | while | flops 1325961472 | bytes 4130527 | solution.py:54
  118.1 4.0 %fusion.33 = bf16[7,96,1024]{2,1,0:T(8,128)(2,1)S(1)} fusion(bf16[7,96,1024]{2,1,0:T(8,128)(2,1)S(1)} %get-tuple-element.336, s32[]{:T(128)S(6)} %select_n.27, f32[128,1536]{1,0:T(8,128)S(1)} %multiply_multiply_fusion.2, bf16[384,1536]{1,0:T(8,128)(2,1)} %get-tuple-element.357, bf16[7,384,1024]{2,1,0:T(8,128)(2,1)} %get-tuple-element.356, ...), kind=kOutput, calls=%fused_computation.7.clone.1 | convolution fusion | flops 1324388352 | bytes 3298816 | tf_op jit(solution)/shard_map/while/body/eval_jaxpr/ltj,mj->lmt/dot_general | solution.py:45
  122.5 4.0 %fusion.33 = bf16[7,96,1024]{2,1,0:T(8,128)(2,1)S(1)} fusion(bf16[7,96,1024]{2,1,0:T(8,128)(2,1)S(1)} %get-tuple-element.336, s32[]{:T(128)S(6)} %select_n.27, f32[128,1536]{1,0:T(8,128)S(1)} %multiply_multiply_fusion.2, bf16[384,1536]{1,0:T(8,128)(2,1)} %get-tuple-element.357, bf16[7,384,1024]{2,1,0:T(8,128)(2,1)} %get-tuple-element.356, ...), kind=kOutput, calls=%fused_computation.7.clone.1 | convolution fusion | flops 1324388352 | bytes 3298816 | tf_op jit(solution)/shard_map/while/body/eval_jaxpr/ltj,mj->lmt/dot_general | solution.py:45
  126.9 4.0 %fusion.33 = bf16[7,96,1024]{2,1,0:T(8,128)(2,1)S(1)} fusion(bf16[7,96,1024]{2,1,0:T(8,128)(2,1)S(1)} %get-tuple-element.336, s32[]{:T(128)S(6)} %select_n.27, f32[128,1536]{1,0:T(8,128)S(1)} %multiply_multiply_fusion.2, bf16[384,1536]{1,0:T(8,128)(2,1)} %get-tuple-element.357, bf16[7,384,1024]{2,1,0:T(8,128)(2,1)} %get-tuple-element.356, ...), kind=kOutput, calls=%fused_computation.7.clone.1 | convolution fusion | flops 1324388352 | bytes 3298816 | tf_op jit(solution)/shard_map/while/body/eval_jaxpr/ltj,mj->lmt/dot_general | solution.py:45
  131.2 4.0 %fusion.33 = bf16[7,96,1024]{2,1,0:T(8,128)(2,1)S(1)} fusion(bf16[7,96,1024]{2,1,0:T(8,128)(2,1)S(1)} %get-tuple-element.336, s32[]{:T(128)S(6)} %select_n.27, f32[128,1536]{1,0:T(8,128)S(1)} %multiply_multiply_fusion.2, bf16[384,1536]{1,0:T(8,128)(2,1)} %get-tuple-element.357, bf16[7,384,1024]{2,1,0:T(8,128)(2,1)} %get-tuple-element.356, ...), kind=kOutput, calls=%fused_computation.7.clone.1 | convolution fusion | flops 1324388352 | bytes 3298816 | tf_op jit(solution)/shard_map/while/body/eval_jaxpr/ltj,mj->lmt/dot_general | solution.py:45
  135.6 4.0 %fusion.33 = bf16[7,96,1024]{2,1,0:T(8,128)(2,1)S(1)} fusion(bf16[7,96,1024]{2,1,0:T(8,128)(2,1)S(1)} %get-tuple-element.336, s32[]{:T(128)S(6)} %select_n.27, f32[128,1536]{1,0:T(8,128)S(1)} %multiply_multiply_fusion.2, bf16[384,1536]{1,0:T(8,128)(2,1)} %get-tuple-element.357, bf16[7,384,1024]{2,1,0:T(8,128)(2,1)} %get-tuple-element.356, ...), kind=kOutput, calls=%fused_computation.7.clone.1 | convolution fusion | flops 1324388352 | bytes 3298816 | tf_op jit(solution)/shard_map/while/body/eval_jaxpr/ltj,mj->lmt/dot_general | solution.py:45
  140.0 4.0 %fusion.33 = bf16[7,96,1024]{2,1,0:T(8,128)(2,1)S(1)} fusion(bf16[7,96,1024]{2,1,0:T(8,128)(2,1)S(1)} %get-tuple-element.336, s32[]{:T(128)S(6)} %select_n.27, f32[128,1536]{1,0:T(8,128)S(1)} %multiply_multiply_fusion.2, bf16[384,1536]{1,0:T(8,128)(2,1)} %get-tuple-element.357, bf16[7,384,1024]{2,1,0:T(8,128)(2,1)} %get-tuple-element.356, ...), kind=kOutput, calls=%fused_computation.7.clone.1 | convolution fusion | flops 1324388352 | bytes 3298816 | tf_op jit(solution)/shard_map/while/body/eval_jaxpr/ltj,mj->lmt/dot_general | solution.py:45
  144.3 4.0 %fusion.33 = bf16[7,96,1024]{2,1,0:T(8,128)(2,1)S(1)} fusion(bf16[7,96,1024]{2,1,0:T(8,128)(2,1)S(1)} %get-tuple-element.336, s32[]{:T(128)S(6)} %select_n.27, f32[128,1536]{1,0:T(8,128)S(1)} %multiply_multiply_fusion.2, bf16[384,1536]{1,0:T(8,128)(2,1)} %get-tuple-element.357, bf16[7,384,1024]{2,1,0:T(8,128)(2,1)} %get-tuple-element.356, ...), kind=kOutput, calls=%fused_computation.7.clone.1 | convolution fusion | flops 1324388352 | bytes 3298816 | tf_op jit(solution)/shard_map/while/body/eval_jaxpr/ltj,mj->lmt/dot_general | solution.py:45
  148.7 4.0 %fusion.33 = bf16[7,96,1024]{2,1,0:T(8,128)(2,1)S(1)} fusion(bf16[7,96,1024]{2,1,0:T(8,128)(2,1)S(1)} %get-tuple-element.336, s32[]{:T(128)S(6)} %select_n.27, f32[128,1536]{1,0:T(8,128)S(1)} %multiply_multiply_fusion.2, bf16[384,1536]{1,0:T(8,128)(2,1)} %get-tuple-element.357, bf16[7,384,1024]{2,1,0:T(8,128)(2,1)} %get-tuple-element.356, ...), kind=kOutput, calls=%fused_computation.7.clone.1 | convolution fusion | flops 1324388352 | bytes 3298816 | tf_op jit(solution)/shard_map/while/body/eval_jaxpr/ltj,mj->lmt/dot_general | solution.py:45
  152.7 1.1 copy-done.2
  (74 shorter events, 6.1 us)
Async XLA Ops:
  7.2 9.3 %copy-start = (f32[7]{0:T(128)S(1)}, f32[7]{0:T(128)}, u32[]{:S(2)}) copy-start(f32[7]{0:T(128)} %param.9) | copy-start | bytes 88
  7.2 36.1 %all-reduce.4.cloned.1.call-start = ((), (), s32[]{:S(2)}) async-start(), calls=%async_computation | async-start | bytes 393216 | tf_op jit(solution)/shard_map/psum | solution.py:64
  15.4 2.6 %copy-start.1 = (bf16[7,96,1024]{2,1,0:T(8,128)(2,1)S(1)}, bf16[7,96,1024]{2,1,0:T(8,128)(2,1)}, u32[]{:S(2)}) copy-start(bf16[7,96,1024]{2,1,0:T(8,128)(2,1)} %param.8) | copy-start | bytes 4128772
  18.0 80.5 %all-gather.6.cloned.1.call-start = ((), (), s32[]{:S(2)}) async-start(), calls=%async_computation.2 | async-start | bytes 6881280 | tf_op jit(solution)/shard_map/all_gather | solution.py:95
  56.5 0.7 copy-start.5
  56.5 0.7 copy-start.6
  56.5 15.1 %copy-start.3 = (f32[96,512]{1,0:T(8,128)S(1)}, f32[96,512]{1,0:T(8,128)}, u32[]{:S(2)}) copy-start(f32[96,512]{1,0:T(8,128)} %all-reduce.4.cloned.1.call-done) | copy-start | bytes 589828
  56.5 15.1 %copy-start.4 = (f32[96,512]{1,0:T(8,128)S(1)}, f32[96,512]{1,0:T(8,128)}, u32[]{:S(2)}) copy-start(f32[96,512]{1,0:T(8,128)} %param.13) | copy-start | bytes 589828
  56.6 61.0 %all-gather.4.cloned.1.call-start = ((), (), s32[]{:S(2)}) async-start(), calls=%async_computation.1 | async-start | bytes 1474560 | tf_op jit(solution)/shard_map/all_gather | solution.py:96
  71.8 4.5 %collective-permute-start = (bf16[192,512]{1,0:T(8,128)(2,1)S(1)}, bf16[192,512]{1,0:T(8,128)(2,1)S(1)}, u32[]{:S(2)}, u32[]{:S(2)}) collective-permute-start(bf16[192,512]{1,0:T(8,128)(2,1)S(1)} %pad_maximum_fusion.1), channel_id=1, source_target_pairs={{0,8},{8,16},{16,24},{1,9},{9,17},{17,25},{2,10},{10,18},{18,26},{... | collective-permute-start | bytes 589832 | tf_op jit(solution)/shard_map/ppermute | solution.py:17
  73.1 7.6 %collective-permute-start.1 = (bf16[192,512]{1,0:T(8,128)(2,1)S(1)}, bf16[192,512]{1,0:T(8,128)(2,1)S(1)}, u32[]{:S(2)}, u32[]{:S(2)}) collective-permute-start(bf16[192,512]{1,0:T(8,128)(2,1)S(1)} %pad_maximum_fusion.1), channel_id=1, source_target_pairs={{8,0},{16,8},{24,16},{9,1},{17,9},{25,17},{10,2},{18,10},{26,18},{... | collective-permute-start | bytes 589832 | tf_op jit(solution)/shard_map/ppermute | solution.py:18
  81.5 4.0 %collective-permute-start.2 = (f32[2,512]{1,0:T(2,128)S(1)}, f32[2,512]{1,0:T(2,128)S(1)}, u32[]{:S(2)}, u32[]{:S(2)}) collective-permute-start(f32[2,512]{1,0:T(2,128)S(1)} %pad_maximum_fusion.3), channel_id=1, source_target_pairs={{0,8},{8,16},{16,24},{1,9},{9,17},{17,25},{2,10},{10,18},{18,26},{... | collective-permute-start | bytes 12296 | tf_op jit(solution)/shard_map/ppermute | solution.py:17
  84.2 5.5 %collective-permute-start.3 = (f32[2,512]{1,0:T(2,128)S(1)}, f32[2,512]{1,0:T(2,128)S(1)}, u32[]{:S(2)}, u32[]{:S(2)}) collective-permute-start(f32[2,512]{1,0:T(2,128)S(1)} %pad_maximum_fusion.3), channel_id=1, source_target_pairs={{8,0},{16,8},{24,16},{9,1},{17,9},{25,17},{10,2},{18,10},{26,18},{... | collective-permute-start | bytes 12296 | tf_op jit(solution)/shard_map/ppermute | solution.py:18
  152.7 1.1 copy-start.2
Sparse Core Ops, SparseCore 0:
  18.1 25.1 all-reduce.3
  56.7 41.7 all-gather.5
  100.1 17.4 all-gather.3
